TPU v7x, 32 devices: a whole 2x2x4 slice. The times are simulated.
32 devices in a mesh: dp: 16 (over z, y, x), tensor: 2 (over core).
Axes of the slice: x: 2, y: 2, z: 4, core: 2. Of those that a mesh axis runs over, the one named last changes fastest.
Arguments:
- inputs: bfloat16 [4, 8192, 768], P(None, ('dp', 'tensor')), may hold values from -6 to 6
- lengths: int32 [4, 16], P(None, 'dp'), may hold values from 128 to 512, as said below
- bounds: int32 [4, 16], P(None, 'dp'), may hold values from 32 to 384, as said below
- query_matrix: bfloat16 [768, 768], P('dp', 'tensor'), may hold values from -0.21875 to 0.21875
- key_matrix: bfloat16 [768, 768], P('dp', 'tensor'), may hold values from -0.21875 to 0.21875
- value_matrix: bfloat16 [768, 768], P('dp', 'tensor'), may hold values from -0.21875 to 0.21875
- query_value_bias: float32 [2, 768], P(None, 'tensor'), may hold values from -3 to 3
- adapter_down_weight: bfloat16 [2, 768, 8], P(None, 'dp'), may hold values from -0.21875 to 0.21875
- adapter_up_weight: bfloat16 [2, 8, 768], P(None, None, 'tensor'), may hold values from -1 to 1
- attention_output_weight: bfloat16 [768, 768], P('tensor', 'dp'), may hold values from -1.75 to 1.75
- feedforward_input_weight: bfloat16 [768, 3072], P('dp', 'tensor'), may hold values from -0.21875 to 0.21875
- feedforward_input_bias: float32 [3072], P('tensor'), may hold values from -3 to 3
- feedforward_output_weight: bfloat16 [3072, 768], P('tensor', 'dp'), may hold values from -0.109375 to 0.109375
- output_bias: float32 [2, 768], replicated, may hold values from -3 to 3
- layernorm_scale: float32 [2, 768], replicated, may hold values from 0.5 to 1.5
- layernorm_bias: float32 [2, 768], replicated, may hold values from -2 to 2
- output_gradient: bfloat16 [4, 8192, 768], P(None, ('dp', 'tensor')), may hold values from -6 to 6
Outputs:
- outputs: bfloat16 [4, 8192, 768], P(None, ('dp', 'tensor'))
- input_grad: float32 [4, 8192, 768], P(None, ('dp', 'tensor'))
- lora_up_grad: float32 [2, 8, 768], P(None, None, 'tensor')
Inputs may be any that keep to these rules, and one draw needn't show every extreme that they name: Item i of micro-batch m has live positions 0 to lengths[m, i] - 1 of its 512; the others are padding. An item's first segment is positions 0 to bounds - 1, its second bounds to 511; bounds lies between lengths // 4 and 3 * lengths // 4.
All inputs are finite; a program needn't handle non-finite values.
Results may differ from a plain program's by a relative error of at most 0.015.
The roundings to bfloat16 on the way count: a program that leaves them out, or rounds other values in their place, can miss the bound.
Values may be sent and summed in bfloat16 or wider, within the bound.
No kernel may reach another device: no remote copies, remote signals or barrier semaphores. Data moves between devices by JAX's collectives and lax.ppermute only.
A program may use at most 192 MiB of HBM per device.

v0:
```python
import jax
import jax.numpy as jnp
from jax import lax
from jax.sharding import PartitionSpec as P

HEAD_DIM = 64
UPDATE_RANK = 8
SLOT = 512
adapter_scale = 2.0
masked_value = -1000000000.0
norm_eps = 1e-05
highest_precision = lax.Precision.HIGHEST


def layer_norm(value_rows, gain, shift):
    centre = value_rows - jnp.mean(value_rows, axis=-1, keepdims=True)
    spread = jnp.mean(centre * centre, axis=-1, keepdims=True)
    return centre * lax.rsqrt(spread + norm_eps) * gain + shift


def exact_gelu(value_rows):
    return jax.nn.gelu(value_rows, approximate=False)


def item_mask(length, bound):
    places = jnp.arange(SLOT)
    segment = places >= bound
    return (places < length)[None, :] & (segment[:, None] == segment[None, :])


def split_heads(input_array):
    return input_array.reshape(input_array.shape[0], input_array.shape[1] // HEAD_DIM, HEAD_DIM)


def item_scores(query_heads, key_heads, length, bound):
    scores = (
        jnp.einsum("qhd,khd->hqk", query_heads, key_heads, preferred_element_type=jnp.float32)
        * 0.125
    )
    return jnp.where(item_mask(length, bound)[None], scores, masked_value)


def attend_forward(pieces):
    query_rows, keys, value_rows, length, bound = pieces
    query_heads = split_heads(query_rows)
    value_heads = split_heads(value_rows)
    scores = item_scores(query_heads, split_heads(keys), length, bound)
    peak = jnp.max(scores, axis=-1, keepdims=True)
    totals = jnp.log(jnp.sum(jnp.exp(scores - peak), axis=-1, keepdims=True)) + peak
    soft_weights = jnp.exp(scores - totals).astype(jnp.bfloat16)
    mixed = jnp.einsum(
        "hqk,khd->qhd", soft_weights, value_heads, preferred_element_type=jnp.float32
    )
    return (mixed.reshape(SLOT, query_rows.shape[1]).astype(jnp.bfloat16), totals)


def attend_backward(pieces):
    query_rows, keys, value_rows, grad_mixed, totals, length, bound = pieces
    query_heads = split_heads(query_rows)
    key_heads = split_heads(keys)
    grad_heads = split_heads(grad_mixed)
    scores = item_scores(query_heads, key_heads, length, bound)
    probs = jnp.exp(scores - totals)
    value_gradient = jnp.einsum(
        "hqk,qhd->khd", probs.astype(jnp.bfloat16), grad_heads, preferred_element_type=jnp.float32
    )
    grad_probs = jnp.einsum(
        "qhd,khd->hqk", grad_heads, split_heads(value_rows), preferred_element_type=jnp.float32
    )
    inner = jnp.sum(probs * grad_probs, axis=-1, keepdims=True)
    grad_scores = (probs * (grad_probs - inner)).astype(jnp.bfloat16)
    query_gradient = (
        jnp.einsum("hqk,khd->qhd", grad_scores, key_heads, preferred_element_type=jnp.float32)
        * 0.125
    )
    key_gradient = (
        jnp.einsum("hqk,qhd->khd", grad_scores, query_heads, preferred_element_type=jnp.float32)
        * 0.125
    )
    width = query_rows.shape[1]
    return (
        query_gradient.reshape(SLOT, width).astype(jnp.bfloat16),
        key_gradient.reshape(SLOT, width).astype(jnp.bfloat16),
        value_gradient.reshape(SLOT, width).astype(jnp.bfloat16),
    )


def contract_trailing(left, right):
    return lax.dot_general(
        left, right, (((1,), (1,)), ((), ())), preferred_element_type=jnp.float32
    )


def project_row_batch(
    input_rows,
    query_projected,
    key_projected,
    value_projected,
    down_projected,
    query_value_bias,
    adapter_up_weight,
):
    up_weight_float = adapter_up_weight.astype(jnp.float32)
    lowrank_update = jnp.einsum(
        "td,zdr->ztr", input_rows, down_projected, preferred_element_type=jnp.float32
    )
    query_rows = (
        jnp.dot(input_rows, query_projected, preferred_element_type=jnp.float32)
        + query_value_bias[0]
        + adapter_scale
        * jnp.dot(lowrank_update[0], up_weight_float[0], precision=highest_precision)
    ).astype(jnp.bfloat16)
    keys = jnp.dot(input_rows, key_projected, preferred_element_type=jnp.float32).astype(
        jnp.bfloat16
    )
    value_rows = (
        jnp.dot(input_rows, value_projected, preferred_element_type=jnp.float32)
        + query_value_bias[1]
        + adapter_scale
        * jnp.dot(lowrank_update[1], up_weight_float[1], precision=highest_precision)
    ).astype(jnp.bfloat16)
    return (lowrank_update, query_rows, keys, value_rows)


def adapter_components(lowrank_update, query_gradient, value_gradient):
    first_dims = (((0,), (0,)), ((), ()))
    return adapter_scale * jnp.stack(
        [
            lax.dot_general(
                lowrank_update[0],
                query_gradient.astype(jnp.float32),
                first_dims,
                precision=highest_precision,
            ),
            lax.dot_general(
                lowrank_update[1],
                value_gradient.astype(jnp.float32),
                first_dims,
                precision=highest_precision,
            ),
        ]
    )


def input_terms_all(
    query_gradient,
    key_gradient,
    value_gradient,
    query_projected,
    key_projected,
    value_projected,
    down_projected,
    adapter_up_weight,
):
    query_lowrank_gradient = adapter_scale * contract_trailing(query_gradient, adapter_up_weight[0])
    value_lowrank_gradient = adapter_scale * contract_trailing(value_gradient, adapter_up_weight[1])
    down_float = down_projected.astype(jnp.float32)
    total = contract_trailing(query_gradient, query_projected)
    total = total + contract_trailing(key_gradient, key_projected)
    total = total + contract_trailing(value_gradient, value_projected)
    total = total + lax.dot_general(
        query_lowrank_gradient, down_float[0], (((1,), (1,)), ((), ())), precision=highest_precision
    )
    total = total + lax.dot_general(
        value_lowrank_gradient, down_float[1], (((1,), (1,)), ((), ())), precision=highest_precision
    )
    return total


def forward_pass(rows_local, item_lengths, item_bounds, gathered, parameters):
    (
        query_projected,
        key_projected,
        value_projected,
        down_projected,
        out_full,
        ffn_in_full,
        ffn_out_full,
    ) = gathered
    (
        query_value_bias,
        adapter_up_weight,
        feedforward_input_bias,
        output_bias,
        layernorm_scale,
        layernorm_bias,
    ) = parameters
    group_items = item_lengths.shape[0]
    row_groups = lax.all_gather(rows_local, "tensor", axis=0, tiled=True)
    lowrank_update, query_rows, keys, value_rows = project_row_batch(
        row_groups,
        query_projected,
        key_projected,
        value_projected,
        down_projected,
        query_value_bias,
        adapter_up_weight,
    )
    width = query_rows.shape[1]
    item_shape = (group_items, SLOT, width)
    mixed, totals = lax.map(
        attend_forward,
        (
            query_rows.reshape(item_shape),
            keys.reshape(item_shape),
            value_rows.reshape(item_shape),
            item_lengths,
            item_bounds,
        ),
    )
    mixed_rows = mixed.reshape(group_items * SLOT, width)
    attended = lax.psum_scatter(
        jnp.dot(mixed_rows, out_full, preferred_element_type=jnp.float32),
        "tensor",
        scatter_dimension=0,
        tiled=True,
    )
    hidden_sum = rows_local.astype(jnp.float32) + attended + output_bias[0]
    normed = layer_norm(hidden_sum, layernorm_scale[0], layernorm_bias[0])
    pre_act = (
        jnp.dot(
            lax.all_gather(normed.astype(jnp.bfloat16), "tensor", axis=0, tiled=True),
            ffn_in_full,
            preferred_element_type=jnp.float32,
        )
        + feedforward_input_bias
    )
    activated = exact_gelu(pre_act).astype(jnp.bfloat16)
    ffn_total = (
        normed
        + lax.psum_scatter(
            jnp.dot(activated, ffn_out_full, preferred_element_type=jnp.float32),
            "tensor",
            scatter_dimension=0,
            tiled=True,
        )
        + output_bias[1]
    )
    result = layer_norm(ffn_total, layernorm_scale[1], layernorm_bias[1]).astype(jnp.bfloat16)
    kept = (lowrank_update, query_rows, keys, value_rows, totals, hidden_sum, pre_act, ffn_total)
    return (result, kept)


def layer_backward(grad_out, item_lengths, item_bounds, gathered, parameters, kept):
    (
        query_projected,
        key_projected,
        value_projected,
        down_projected,
        out_full,
        ffn_in_full,
        ffn_out_full,
    ) = gathered
    (
        query_value_bias,
        adapter_up_weight,
        feedforward_input_bias,
        output_bias,
        layernorm_scale,
        layernorm_bias,
    ) = parameters
    lowrank_update, query_rows, keys, value_rows, totals, hidden_sum, pre_act, ffn_total = kept
    group_items = item_lengths.shape[0]
    outer_pull = jax.vjp(
        lambda field: layer_norm(field, layernorm_scale[1], layernorm_bias[1]), ffn_total
    )[1]
    grad_sum = outer_pull(grad_out.astype(jnp.float32))[0]
    grad_act = contract_trailing(
        lax.all_gather(grad_sum.astype(jnp.bfloat16), "tensor", axis=0, tiled=True), ffn_out_full
    )
    gelu_pull = jax.vjp(exact_gelu, pre_act)[1]
    grad_pre = gelu_pull(grad_act)[0].astype(jnp.bfloat16)
    grad_normed = grad_sum + lax.psum_scatter(
        contract_trailing(grad_pre, ffn_in_full), "tensor", scatter_dimension=0, tiled=True
    )
    inner_pull = jax.vjp(
        lambda field: layer_norm(field, layernorm_scale[0], layernorm_bias[0]), hidden_sum
    )[1]
    grad_hidden = inner_pull(grad_normed)[0]
    grad_mixed = contract_trailing(
        lax.all_gather(grad_hidden.astype(jnp.bfloat16), "tensor", axis=0, tiled=True), out_full
    ).astype(jnp.bfloat16)
    width = query_rows.shape[1]
    item_shape = (group_items, SLOT, width)
    query_gradient, key_gradient, value_gradient = lax.map(
        attend_backward,
        (
            query_rows.reshape(item_shape),
            keys.reshape(item_shape),
            value_rows.reshape(item_shape),
            grad_mixed.reshape(item_shape),
            totals,
            item_lengths,
            item_bounds,
        ),
    )
    query_gradient = query_gradient.reshape(group_items * SLOT, width)
    key_gradient = key_gradient.reshape(group_items * SLOT, width)
    value_gradient = value_gradient.reshape(group_items * SLOT, width)
    adapter_portion = adapter_components(lowrank_update, query_gradient, value_gradient)
    row_gradient = grad_hidden + lax.psum_scatter(
        input_terms_all(
            query_gradient,
            key_gradient,
            value_gradient,
            query_projected,
            key_projected,
            value_projected,
            down_projected,
            adapter_up_weight,
        ).astype(jnp.bfloat16),
        "tensor",
        scatter_dimension=0,
        tiled=True,
    ).astype(jnp.float32)
    return (row_gradient, adapter_portion)


def local(
    inputs,
    lengths,
    bounds,
    query_matrix,
    key_matrix,
    value_matrix,
    query_value_bias,
    adapter_down_weight,
    adapter_up_weight,
    attention_output_weight,
    feedforward_input_weight,
    feedforward_input_bias,
    feedforward_output_weight,
    output_bias,
    layernorm_scale,
    layernorm_bias,
    output_gradient,
):
    micro_count = inputs.shape[0]
    parameters = (
        query_value_bias,
        adapter_up_weight,
        feedforward_input_bias,
        output_bias,
        layernorm_scale,
        layernorm_bias,
    )
    result_list = []
    gradient_tree = []
    adapter_combined = jnp.zeros((2, UPDATE_RANK, adapter_up_weight.shape[2]), jnp.float32)
    for batch_index in range(micro_count):
        forward_set = (
            lax.all_gather(query_matrix, "dp", axis=0, tiled=True),
            lax.all_gather(key_matrix, "dp", axis=0, tiled=True),
            lax.all_gather(value_matrix, "dp", axis=0, tiled=True),
            lax.all_gather(adapter_down_weight, "dp", axis=1, tiled=True),
            lax.all_gather(attention_output_weight, "dp", axis=1, tiled=True),
            lax.all_gather(feedforward_input_weight, "dp", axis=0, tiled=True),
            lax.all_gather(feedforward_output_weight, "dp", axis=1, tiled=True),
        )
        result, kept = forward_pass(
            inputs[batch_index], lengths[batch_index], bounds[batch_index], forward_set, parameters
        )
        backward_set = (
            lax.all_gather(query_matrix, "dp", axis=0, tiled=True),
            lax.all_gather(key_matrix, "dp", axis=0, tiled=True),
            lax.all_gather(value_matrix, "dp", axis=0, tiled=True),
            lax.all_gather(adapter_down_weight, "dp", axis=1, tiled=True),
            lax.all_gather(attention_output_weight, "dp", axis=1, tiled=True),
            lax.all_gather(feedforward_input_weight, "dp", axis=0, tiled=True),
            lax.all_gather(feedforward_output_weight, "dp", axis=1, tiled=True),
        )
        row_gradient, adapter_portion = layer_backward(
            output_gradient[batch_index],
            lengths[batch_index],
            bounds[batch_index],
            backward_set,
            parameters,
            kept,
        )
        adapter_combined = adapter_combined + lax.psum(adapter_portion, "dp")
        result_list.append(result)
        gradient_tree.append(row_gradient)
    return (jnp.stack(result_list), jnp.stack(gradient_tree), adapter_combined)


def solution(mesh):
    return jax.shard_map(
        local,
        mesh=mesh,
        in_specs=(
            P(None, ("dp", "tensor"), None),
            P(None, "dp"),
            P(None, "dp"),
            P("dp", "tensor"),
            P("dp", "tensor"),
            P("dp", "tensor"),
            P(None, "tensor"),
            P(None, "dp", None),
            P(None, None, "tensor"),
            P("tensor", "dp"),
            P("dp", "tensor"),
            P("tensor"),
            P("tensor", "dp"),
            P(),
            P(),
            P(),
            P(None, ("dp", "tensor"), None),
        ),
        out_specs=(
            P(None, ("dp", "tensor"), None),
            P(None, ("dp", "tensor"), None),
            P(None, None, "tensor"),
        ),
        check_vma=False,
    )
```

profile of v0, /device:TPU:0, one launch (start us, length us, event | category | flops | bytes accessed | tf_op | source)
XLA Modules:
  0.0 771.6 jit_solution(13941130316083166364)
XLA Ops:
  12.5 44.5 %all_gather.48 = bf16[2,768,8]{2,0,1:T(2,128)(2,1)S(1)} all-gather(bf16[2,48,8]{2,0,1:T(2,128)(2,1)S(1)} %copy.57), channel_id=1, replica_groups=mesh['dp'=16,'tensor'=2] {'dp'}, dimensions={1}, use_global_device_ids=true | all-gather | bytes 26112 | tf_op jit(solution)/shard_map/all_gather | solution.py:355
  57.3 39.2 %all_gather.49 = bf16[768,384]{1,0:T(8,128)(2,1)S(1)} all-gather(bf16[48,384]{1,0:T(8,128)(2,1)} %param.20), channel_id=1, replica_groups=mesh['dp'=16,'tensor'=2] {'dp'}, dimensions={0}, use_global_device_ids=true | all-gather | bytes 626688 | tf_op jit(solution)/shard_map/all_gather | solution.py:352
  96.5 41.1 %all_gather.50 = bf16[768,384]{1,0:T(8,128)(2,1)S(1)} all-gather(bf16[48,384]{1,0:T(8,128)(2,1)} %param.21), channel_id=1, replica_groups=mesh['dp'=16,'tensor'=2] {'dp'}, dimensions={0}, use_global_device_ids=true | all-gather | bytes 626688 | tf_op jit(solution)/shard_map/all_gather | solution.py:353
  137.5 39.3 %all_gather.47 = bf16[768,384]{1,0:T(8,128)(2,1)S(1)} all-gather(bf16[48,384]{1,0:T(8,128)(2,1)} %param.22), channel_id=1, replica_groups=mesh['dp'=16,'tensor'=2] {'dp'}, dimensions={0}, use_global_device_ids=true | all-gather | bytes 626688 | tf_op jit(solution)/shard_map/all_gather | solution.py:354
  176.8 40.8 %all_gather.51 = bf16[384,768]{0,1:T(8,128)(2,1)S(1)} all-gather(bf16[384,48]{0,1:T(8,128)(2,1)} %param.26), channel_id=1, replica_groups=mesh['dp'=16,'tensor'=2] {'dp'}, dimensions={1}, use_global_device_ids=true | all-gather | bytes 626688 | tf_op jit(solution)/shard_map/all_gather | solution.py:356
  280.6 4.3 fusion.188
  289.5 47.2 %all-gather.7.cloned.1.call-done = bf16[768,1536]{1,0:T(8,128)(2,1)} async-done(((bf16[48,1536]{1,0:T(8,128)(2,1)}), bf16[768,1536]{1,0:T(8,128)(2,1)}) %all-gather.7.cloned.1.call-update) | async-done | bytes 2359312 | tf_op jit(solution)/shard_map/all_gather | solution.py:357
  336.7 10.4 %fusion.11 = (f32[512,1536]{1,0:T(8,128)}, f32[512,1536]{1,0:T(8,128)}) fusion(f32[1536]{0:T(1024)S(1)} %copy-done.198, bf16[512,768]{1,0:T(8,128)(2,1)S(1)} %all_gather.60, bf16[768,1536]{1,0:T(8,128)(2,1)} %all-gather.7.cloned.1.call-done), kind=kOutput, calls=%fused_computation.39 | convolution fusion | flops 1257504768 | bytes 9443328 | tf_op jit(solution)/shard_map/dot_general | solution.py:221
  347.2 52.7 %all-gather.9.cloned.1.call-done = bf16[1536,768]{0,1:T(8,128)(2,1)} async-done(((bf16[1536,48]{0,1:T(8,128)(2,1)}), bf16[1536,768]{0,1:T(8,128)(2,1)}) %all-gather.9.cloned.1.call-update) | async-done | bytes 2359312 | tf_op jit(solution)/shard_map/all_gather | solution.py:358
  399.9 6.1 fusion.35
  408.4 9.7 %fusion.10 = (f32[512,1536]{1,0:T(8,128)S(1)}, f32[512,1536]{1,0:T(8,128)S(1)}) fusion(f32[1536]{0:T(1024)} %param.28, bf16[512,768]{1,0:T(8,128)(2,1)S(1)} %all_gather.58, bf16[768,1536]{1,0:T(8,128)(2,1)} %all-gather.7.cloned.1.call-done), kind=kOutput, calls=%fused_computation.38 | convolution fusion | flops 1257504768 | bytes 9443328 | tf_op jit(solution)/shard_map/dot_general | solution.py:221
  425.9 9.5 %fusion.9 = (f32[512,1536]{1,0:T(8,128)S(1)}, f32[512,1536]{1,0:T(8,128)S(1)}) fusion(f32[1536]{0:T(1024)} %param.28, bf16[512,768]{1,0:T(8,128)(2,1)S(1)} %all_gather.56, bf16[768,1536]{1,0:T(8,128)(2,1)} %all-gather.7.cloned.1.call-done), kind=kOutput, calls=%fused_computation.37 | convolution fusion | flops 1257504768 | bytes 9443328 | tf_op jit(solution)/shard_map/dot_general | solution.py:221
  442.4 5.9 reduce-scatter.23.cloned.1.call-done
  448.4 4.5 fusion.187
  455.2 8.1 %fusion.8 = (f32[512,1536]{1,0:T(8,128)S(1)}, f32[512,1536]{1,0:T(8,128)S(1)}) fusion(f32[1536]{0:T(1024)S(1)} %copy-done.199, bf16[512,768]{1,0:T(8,128)(2,1)S(1)} %all_gather.52, bf16[768,1536]{1,0:T(8,128)(2,1)S(1)} %copy-done.197), kind=kOutput, calls=%fused_computation.36 | convolution fusion | flops 1257504768 | bytes 9443328 | tf_op jit(solution)/shard_map/dot_general | solution.py:221
  468.7 10.4 %reduce-scatter.19.cloned.1.call-done = f32[256,768]{1,0:T(8,128)} async-done(((f32[512,768]{1,0:T(8,128)}), f32[256,768]{1,0:T(8,128)}) %reduce-scatter.19.cloned.1.call-update) | async-done | bytes 786448 | tf_op jit(solution)/shard_map/reduce_scatter | solution.py:231
  489.2 7.8 %fusion.43 = f32[512,768]{1,0:T(8,128)} fusion(bf16[768,1536]{1,0:T(8,128)(2,1)} %all-gather.7.cloned.1.call-done, f32[512,1536]{1,0:T(8,128)} %get-tuple-element.339, f32[512,1536]{1,0:T(8,128)} %get-tuple-element.340, bf16[512,768]{1,0:T(8,128)(2,1)} %all_gather.67, bf16[1536,768]{0,1:T(8,128)(2,1)S(1)} %copy-done.4), kind=kOutput, calls=%fused_computation.117 | convolution fusion | flops 2426929152 | bytes 13369344 | tf_op jit(solution)/shard_map/dot_general | solution.py:89
  499.1 4.4 fusion.181
  507.1 7.8 %fusion.42 = f32[512,768]{1,0:T(8,128)} fusion(bf16[768,1536]{1,0:T(8,128)(2,1)} %all-gather.7.cloned.1.call-done, f32[512,1536]{1,0:T(8,128)} %copy-done.82, f32[512,1536]{1,0:T(8,128)} %copy-done.83, bf16[512,768]{1,0:T(8,128)(2,1)} %all_gather.65, bf16[1536,768]{0,1:T(8,128)(2,1)S(1)} %copy-done.4), kind=kOutput, calls=%fused_computation.116 | convolution fusion | flops 2426929152 | bytes 13369344 | tf_op jit(solution)/shard_map/dot_general | solution.py:89
  519.1 8.3 %fusion.40 = f32[512,768]{1,0:T(8,128)} fusion(bf16[768,1536]{1,0:T(8,128)(2,1)} %all-gather.7.cloned.1.call-done, f32[512,1536]{1,0:T(8,128)} %copy-done.84, f32[512,1536]{1,0:T(8,128)} %copy-done.85, bf16[512,768]{1,0:T(8,128)(2,1)} %all_gather.61, bf16[1536,768]{0,1:T(8,128)(2,1)S(1)} %copy-done.4), kind=kOutput, calls=%fused_computation.114 | convolution fusion | flops 2426929152 | bytes 13369344 | tf_op jit(solution)/shard_map/dot_general | solution.py:89
  531.3 7.8 %fusion.41 = f32[512,768]{1,0:T(8,128)} fusion(bf16[768,1536]{1,0:T(8,128)(2,1)} %all-gather.7.cloned.1.call-done, f32[512,1536]{1,0:T(8,128)} %copy-done.80, f32[512,1536]{1,0:T(8,128)} %copy-done.81, bf16[512,768]{1,0:T(8,128)(2,1)} %all_gather.63, bf16[1536,768]{0,1:T(8,128)(2,1)S(1)} %copy-done.4), kind=kOutput, calls=%fused_computation.115 | convolution fusion | flops 2426929152 | bytes 13369344 | tf_op jit(solution)/shard_map/dot_general | solution.py:89
  545.2 5.8 reduce-scatter.37.cloned.1.call-done
  556.9 4.6 convolution_convert_fusion.6
  588.9 4.6 multiply_reduce_fusion.3
  593.6 6.5 multiply_convert_fusion.3
  603.3 4.8 multiply_reduce_fusion.2
  608.2 4.7 multiply_reduce_fusion.1
  612.8 5.6 multiply_reduce_fusion
  622.1 6.7 multiply_convert_fusion.2
  630.5 4.9 multiply_convert_fusion.1
  637.3 4.7 multiply_convert_fusion
  676.5 77.1 %psum.34 = f32[2,8,384]{2,1,0:T(8,128)} all-reduce(f32[2,8,384]{2,1,0:T(8,128)S(1)} %fusion.110), channel_id=1, replica_groups=mesh['dp'=16,'tensor'=2] {'dp'}, use_global_device_ids=true, to_apply=%region_60.61 | all-reduce | flops 6144 | bytes 49152 | tf_op jit(solution)/shard_map/psum | solution.py:380
  (670 shorter events, 213.0 us)
Async XLA Ops:
  8.0 270.0 %reduce-scatter.21.cloned.1.call-start = ((), (), s32[]{:S(2)}) async-start(), calls=%async_computation.20 | async-start | bytes 2359296 | tf_op jit(solution)/shard_map/reduce_scatter | solution.py:212
  57.3 207.3 %copy-start.88 = (bf16[2,768,8]{1,2,0:T(8,128)(2,1)}, bf16[2,768,8]{1,2,0:T(8,128)(2,1)S(1)}, u32[]{:S(2)}) copy-start(bf16[2,768,8]{1,2,0:T(8,128)(2,1)S(1)} %copy.58) | copy-start | bytes 73732
  57.3 160.3 %copy-start.53 = (bf16[4,256,768]{2,1,0:T(8,128)(2,1)S(1)}, bf16[4,256,768]{2,1,0:T(8,128)(2,1)}, u32[]{:S(2)}) copy-start(bf16[4,256,768]{2,1,0:T(8,128)(2,1)} %param.17) | copy-start | bytes 4718596
  96.5 168.4 %copy-start.19 = (bf16[768,384]{1,0:T(8,128)(2,1)}, bf16[768,384]{1,0:T(8,128)(2,1)S(1)}, u32[]{:S(2)}) copy-start(bf16[768,384]{1,0:T(8,128)(2,1)S(1)} %all_gather.49) | copy-start | bytes 1769476
  137.5 129.9 %copy-start.14 = (bf16[768,384]{1,0:T(8,128)(2,1)}, bf16[768,384]{1,0:T(8,128)(2,1)S(1)}, u32[]{:S(2)}) copy-start(bf16[768,384]{1,0:T(8,128)(2,1)S(1)} %all_gather.50) | copy-start | bytes 1769476
  176.8 93.8 %copy-start.22 = (bf16[768,384]{1,0:T(8,128)(2,1)}, bf16[768,384]{1,0:T(8,128)(2,1)S(1)}, u32[]{:S(2)}) copy-start(bf16[768,384]{1,0:T(8,128)(2,1)S(1)} %all_gather.47) | copy-start | bytes 1769476
  217.6 56.1 %copy-start.24 = (bf16[384,768]{0,1:T(8,128)(2,1)}, bf16[384,768]{0,1:T(8,128)(2,1)S(1)}, u32[]{:S(2)}) copy-start(bf16[384,768]{0,1:T(8,128)(2,1)S(1)} %all_gather.51) | copy-start | bytes 1769476
  232.9 45.1 %reduce-scatter.17.cloned.1.call-start = ((), (), s32[]{:S(2)}) async-start(), calls=%async_computation.16 | async-start | bytes 2359296 | tf_op jit(solution)/shard_map/reduce_scatter | solution.py:212
  247.3 30.7 %reduce-scatter.29.cloned.1.call-start = ((), (), s32[]{:S(2)}) async-start(), calls=%async_computation.24 | async-start | bytes 2359296 | tf_op jit(solution)/shard_map/reduce_scatter | solution.py:212
  261.3 19.3 %reduce-scatter.25.cloned.1.call-start = ((), (), s32[]{:S(2)}) async-start(), calls=%async_computation.22 | async-start | bytes 2359296 | tf_op jit(solution)/shard_map/reduce_scatter | solution.py:212
  275.5 61.2 %all-gather.7.cloned.1.call-start = ((), (), s32[]{:S(2)}) async-start(), calls=%async_computation.17 | async-start | bytes 2506752 | tf_op jit(solution)/shard_map/all_gather | solution.py:357
  276.1 123.8 %all-gather.9.cloned.1.call-start = ((), (), s32[]{:S(2)}) async-start(), calls=%async_computation.18 | async-start | bytes 2506752 | tf_op jit(solution)/shard_map/all_gather | solution.py:358
  276.7 165.7 %reduce-scatter.31.cloned.1.call-start = ((), (), s32[]{:S(2)}) async-start(), calls=%async_computation.25 | async-start | bytes 2359296 | tf_op jit(solution)/shard_map/reduce_scatter | solution.py:231
  285.1 51.6 %copy-start.198 = (f32[1536]{0:T(1024)S(1)}, f32[1536]{0:T(1024)}, u32[]{:S(2)}) copy-start(f32[1536]{0:T(1024)} %param.28) | copy-start | bytes 18436
  406.0 36.4 %reduce-scatter.27.cloned.1.call-start = ((), (), s32[]{:S(2)}) async-start(), calls=%async_computation.23 | async-start | bytes 2359296 | tf_op jit(solution)/shard_map/reduce_scatter | solution.py:231
  423.4 24.9 %reduce-scatter.23.cloned.1.call-start = ((), (), s32[]{:S(2)}) async-start(), calls=%async_computation.21 | async-start | bytes 2359296 | tf_op jit(solution)/shard_map/reduce_scatter | solution.py:231
  440.7 38.3 %reduce-scatter.19.cloned.1.call-start = ((), (), s32[]{:S(2)}) async-start(), calls=%async_computation.19 | async-start | bytes 2359296 | tf_op jit(solution)/shard_map/reduce_scatter | solution.py:231
  442.4 36.7 %copy-start.154 = (f32[256]{0:T(256)}, f32[256]{0:T(256)S(1)}, u32[]{:S(2)}) copy-start(f32[256]{0:T(256)S(1)} %fusion.147) | copy-start | bytes 3076
  468.6 73.4 %reduce-scatter.45.cloned.1.call-start = ((), (), s32[]{:S(2)}) async-start(), calls=%async_computation.32 | async-start | bytes 2359296 | tf_op jit(solution)/shard_map/reduce_scatter | solution.py:273
  497.0 45.0 %reduce-scatter.41.cloned.1.call-start = ((), (), s32[]{:S(2)}) async-start(), calls=%async_computation.30 | async-start | bytes 2359296 | tf_op jit(solution)/shard_map/reduce_scatter | solution.py:273
  514.9 27.1 %reduce-scatter.33.cloned.1.call-start = ((), (), s32[]{:S(2)}) async-start(), calls=%async_computation.26 | async-start | bytes 2359296 | tf_op jit(solution)/shard_map/reduce_scatter | solution.py:273
  527.5 23.6 %reduce-scatter.37.cloned.1.call-start = ((), (), s32[]{:S(2)}) async-start(), calls=%async_computation.28 | async-start | bytes 2359296 | tf_op jit(solution)/shard_map/reduce_scatter | solution.py:273
  539.1 214.4 %reduce-scatter.35.cloned.1.call-start = ((), (), s32[]{:S(2)}) async-start(), calls=%async_computation.27 | async-start | bytes 1179648 | tf_op jit(solution)/shard_map/reduce_scatter | solution.py:301
  622.1 133.6 %reduce-scatter.39.cloned.1.call-start = ((), (), s32[]{:S(2)}) async-start(), calls=%async_computation.29 | async-start | bytes 1179648 | tf_op jit(solution)/shard_map/reduce_scatter | solution.py:301
  649.9 107.8 %reduce-scatter.43.cloned.1.call-start = ((), (), s32[]{:S(2)}) async-start(), calls=%async_computation.31 | async-start | bytes 1179648 | tf_op jit(solution)/shard_map/reduce_scatter | solution.py:301
  659.8 100.1 %reduce-scatter.47.cloned.1.call-start = ((), (), s32[]{:S(2)}) async-start(), calls=%async_computation.33 | async-start | bytes 1179648 | tf_op jit(solution)/shard_map/reduce_scatter | solution.py:301
  667.1 86.5 %copy-start.174 = (f32[256]{0:T(256)S(1)}, f32[256]{0:T(256)}, u32[]{:S(2)}) copy-start(f32[256]{0:T(256)} %copy-done.173) | copy-start | bytes 3076
  669.2 84.4 %copy-start.33 = (f32[256,768]{1,0:T(8,128)S(1)}, f32[256,768]{1,0:T(8,128)}, u32[]{:S(2)}) copy-start(f32[256,768]{1,0:T(8,128)} %copy-done.32) | copy-start | bytes 2359300
  669.2 86.4 %copy-start.37 = (f32[256,768]{1,0:T(8,128)S(1)}, f32[256,768]{1,0:T(8,128)}, u32[]{:S(2)}) copy-start(f32[256,768]{1,0:T(8,128)} %copy-done.36) | copy-start | bytes 2359300
  669.2 88.5 %copy-start.35 = (f32[256,768]{1,0:T(8,128)S(1)}, f32[256,768]{1,0:T(8,128)}, u32[]{:S(2)}) copy-start(f32[256,768]{1,0:T(8,128)} %copy-done.34) | copy-start | bytes 2359300
  674.2 85.6 %copy-start.40 = (f32[256,768]{1,0:T(8,128)S(1)}, f32[256,768]{1,0:T(8,128)}, u32[]{:S(2)}) copy-start(f32[256,768]{1,0:T(8,128)} %copy-done.39) | copy-start | bytes 2359300
  674.2 85.6 %copy-start.178 = (f32[256]{0:T(256)S(1)}, f32[256]{0:T(256)}, u32[]{:S(2)}) copy-start(f32[256]{0:T(256)} %copy-done.177) | copy-start | bytes 3076
  (200 other events, 889.0 us)
Sparse Core Ops, SparseCore 0:
  233.0 5.0 reduce-scatter.20
  247.4 5.1 reduce-scatter.16
  261.5 5.1 reduce-scatter.28
  275.6 4.9 reduce-scatter.24
  406.1 7.4 reduce-scatter.30
  423.6 7.4 reduce-scatter.26
  440.8 7.4 reduce-scatter.22
  468.7 10.3 reduce-scatter.18
  497.1 10.3 reduce-scatter.44
  515.0 10.3 reduce-scatter.40
  528.2 10.3 reduce-scatter.32
  540.7 10.3 reduce-scatter.36
  622.2 9.4 reduce-scatter.34
  650.1 9.4 reduce-scatter.38
  661.6 9.2 reduce-scatter.42
  673.6 9.2 reduce-scatter.46
Sparse Core Ops, SparseCore 1:
  278.8 57.9 all-gather.6
  339.4 60.4 all-gather.8
where the time goes:
time: 779 us; the launch traced here: 772 us
  blocking collectives  324 us (42%)
  matrix products  197 us (25%)
  waiting for transfers between devices  126 us (16%)
  other arithmetic  82.3 us (11%)
  local copies, waits for them, and re-layouts  22 us (3%)
  between operations  18.9 us (2%)
    psum x1, blocking collectives, local(): adapter_combined = adapter_combined + lax.psum(adapter_portion, 'dp')  77.1 us
    dot_general x28, matrix products, contract_trailing(): lax.dot_general(left, right, (((1,), (1,)), ((), ())), preferred_element_...  53.7 us
    all_gather x1, waiting for transfers between devices, local(): lax.all_gather(feedforward_output_weight, 'dp', axis=1, tiled=True)  52.7 us
    all_gather x1, waiting for transfers between devices, local(): lax.all_gather(feedforward_input_weight, 'dp', axis=0, tiled=True)  47.2 us
    all_gather x1, blocking collectives, local(): lax.all_gather(adapter_down_weight, 'dp', axis=1, tiled=True)  44.5 us
    all_gather x1, blocking collectives, local(): lax.all_gather(key_matrix, 'dp', axis=0, tiled=True)  41.1 us
    all_gather x1, blocking collectives, local(): lax.all_gather(attention_output_weight, 'dp', axis=1, tiled=True)  40.8 us
    all_gather x1, blocking collectives, local(): lax.all_gather(value_matrix, 'dp', axis=0, tiled=True)  39.3 us
  transfers between devices with their start and end apart: 18, of which 6 were waited for; matrix products, arithmetic and copies ran while one was open for 22% of the time, Pallas kernels for 0%

commit v1 on v0

--- a/solution.py
+++ b/solution.py
@@ -10,6 +10,7 @@
 masked_value = -1000000000.0
 norm_eps = 1e-05
 highest_precision = lax.Precision.HIGHEST
+words_push = lambda x_local, row_axis: jnp.sum(jax.lax.all_gather(x_local, row_axis), 0)
 
 
 def layer_norm(value_rows, gain, shift):
@@ -377,7 +378,7 @@
             parameters,
             kept,
         )
-        adapter_combined = adapter_combined + lax.psum(adapter_portion, "dp")
+        adapter_combined = adapter_combined + words_push(adapter_portion, "dp")
         result_list.append(result)
         gradient_tree.append(row_gradient)
     return (jnp.stack(result_list), jnp.stack(gradient_tree), adapter_combined)

time: 779 us -> 869 us (1.12)
  blocking collectives: 324 us -> 414 us
    all_gather x0 -> x4, blocking collectives: none -> 167 us  [jax.lax.all_gather(x_local, row_axis)]
    psum x1 -> x0, blocking collectives: 77.1 us -> none  [local(): adapter_combined = adapter_combined + lax.psum(adapter_portion, 'dp')]
  transfers between devices with their start and end apart: 18 -> 18, of which waited for: 6 -> 6; matrix products, arithmetic and copies ran while one was open for 22% -> 19% of each run, Pallas kernels for 0% -> 0%
where the time goes in v1:
time: 869 us; the launch traced here: 862 us
  blocking collectives  414 us (48%)
  matrix products  193 us (22%)
  waiting for transfers between devices  128 us (15%)
  other arithmetic  89.1 us (10%)
  local copies, waits for them, and re-layouts  18.5 us (2%)
  between operations  18.5 us (2%)
    all_gather x4, blocking collectives, jax.lax.all_gather(x_local, row_axis)  167 us
    dot_general x28, matrix products, contract_trailing(): lax.dot_general(left, right, (((1,), (1,)), ((), ())), preferred_element_...  55.5 us
    all_gather x1, waiting for transfers between devices, local(): lax.all_gather(feedforward_output_weight, 'dp', axis=1, tiled=True)  52.7 us
    all_gather x1, waiting for transfers between devices, local(): lax.all_gather(feedforward_input_weight, 'dp', axis=0, tiled=True)  47.6 us
    all_gather x1, blocking collectives, local(): lax.all_gather(adapter_down_weight, 'dp', axis=1, tiled=True)  44.5 us
    all_gather x1, blocking collectives, local(): lax.all_gather(key_matrix, 'dp', axis=0, tiled=True)  41.1 us
    all_gather x1, blocking collectives, local(): lax.all_gather(attention_output_weight, 'dp', axis=1, tiled=True)  40.8 us
    all_gather x1, blocking collectives, local(): lax.all_gather(value_matrix, 'dp', axis=0, tiled=True)  39.3 us
  transfers between devices with their start and end apart: 18, of which 6 were waited for; matrix products, arithmetic and copies ran while one was open for 19% of the time, Pallas kernels for 0%

profile of v1, /device:TPU:0, one launch (start us, length us, event | category | flops | bytes accessed | tf_op | source)
XLA Modules:
  0.0 861.9 jit_solution(4652846751452221084)
XLA Ops:
  12.5 44.5 %all_gather.56 = bf16[2,768,8]{2,0,1:T(2,128)(2,1)S(1)} all-gather(bf16[2,48,8]{2,0,1:T(2,128)(2,1)S(1)} %copy.57), channel_id=1, replica_groups=mesh['dp'=16,'tensor'=2] {'dp'}, dimensions={1}, use_global_device_ids=true | all-gather | bytes 26112 | tf_op jit(solution)/shard_map/all_gather | solution.py:356
  57.3 39.2 %all_gather.57 = bf16[768,384]{1,0:T(8,128)(2,1)S(1)} all-gather(bf16[48,384]{1,0:T(8,128)(2,1)} %param.20), channel_id=1, replica_groups=mesh['dp'=16,'tensor'=2] {'dp'}, dimensions={0}, use_global_device_ids=true | all-gather | bytes 626688 | tf_op jit(solution)/shard_map/all_gather | solution.py:353
  96.5 41.1 %all_gather.58 = bf16[768,384]{1,0:T(8,128)(2,1)S(1)} all-gather(bf16[48,384]{1,0:T(8,128)(2,1)} %param.21), channel_id=1, replica_groups=mesh['dp'=16,'tensor'=2] {'dp'}, dimensions={0}, use_global_device_ids=true | all-gather | bytes 626688 | tf_op jit(solution)/shard_map/all_gather | solution.py:354
  137.6 39.3 %all_gather.55 = bf16[768,384]{1,0:T(8,128)(2,1)S(1)} all-gather(bf16[48,384]{1,0:T(8,128)(2,1)} %param.22), channel_id=1, replica_groups=mesh['dp'=16,'tensor'=2] {'dp'}, dimensions={0}, use_global_device_ids=true | all-gather | bytes 626688 | tf_op jit(solution)/shard_map/all_gather | solution.py:355
  176.9 40.8 %all_gather.59 = bf16[384,768]{0,1:T(8,128)(2,1)S(1)} all-gather(bf16[384,48]{0,1:T(8,128)(2,1)} %param.26), channel_id=1, replica_groups=mesh['dp'=16,'tensor'=2] {'dp'}, dimensions={1}, use_global_device_ids=true | all-gather | bytes 626688 | tf_op jit(solution)/shard_map/all_gather | solution.py:357
  289.6 47.6 %all-gather.7.cloned.1.call-done = bf16[768,1536]{1,0:T(8,128)(2,1)} async-done(((bf16[48,1536]{1,0:T(8,128)(2,1)}), bf16[768,1536]{1,0:T(8,128)(2,1)}) %all-gather.7.cloned.1.call-update) | async-done | bytes 2359312 | tf_op jit(solution)/shard_map/all_gather | solution.py:358
  337.2 10.4 %fusion.11 = (f32[512,1536]{1,0:T(8,128)}, f32[512,1536]{1,0:T(8,128)}) fusion(f32[1536]{0:T(1024)S(1)} %copy-done.155, bf16[512,768]{1,0:T(8,128)(2,1)S(1)} %all_gather.68, bf16[768,1536]{1,0:T(8,128)(2,1)} %all-gather.7.cloned.1.call-done), kind=kOutput, calls=%fused_computation.39 | convolution fusion | flops 1257504768 | bytes 9443328 | tf_op jit(solution)/shard_map/dot_general | solution.py:222
  347.6 52.7 %all-gather.9.cloned.1.call-done = bf16[1536,768]{0,1:T(8,128)(2,1)} async-done(((bf16[1536,48]{0,1:T(8,128)(2,1)}), bf16[1536,768]{0,1:T(8,128)(2,1)}) %all-gather.9.cloned.1.call-update) | async-done | bytes 2359312 | tf_op jit(solution)/shard_map/all_gather | solution.py:359
  400.3 6.1 fusion.35
  408.9 9.6 %fusion.10 = (f32[512,1536]{1,0:T(8,128)S(1)}, f32[512,1536]{1,0:T(8,128)S(1)}) fusion(f32[1536]{0:T(1024)S(1)} %copy-done.155, bf16[512,768]{1,0:T(8,128)(2,1)S(1)} %all_gather.66, bf16[768,1536]{1,0:T(8,128)(2,1)} %all-gather.7.cloned.1.call-done), kind=kOutput, calls=%fused_computation.38 | convolution fusion | flops 1257504768 | bytes 9443328 | tf_op jit(solution)/shard_map/dot_general | solution.py:222
  426.5 9.5 %fusion.9 = (f32[512,1536]{1,0:T(8,128)S(1)}, f32[512,1536]{1,0:T(8,128)S(1)}) fusion(f32[1536]{0:T(1024)S(1)} %copy-done.155, bf16[512,768]{1,0:T(8,128)(2,1)S(1)} %all_gather.64, bf16[768,1536]{1,0:T(8,128)(2,1)} %all-gather.7.cloned.1.call-done), kind=kOutput, calls=%fused_computation.37 | convolution fusion | flops 1257504768 | bytes 9443328 | tf_op jit(solution)/shard_map/dot_general | solution.py:222
  443.0 5.9 reduce-scatter.23.cloned.1.call-done
  448.9 4.5 fusion.184
  455.7 8.1 fusion.8
  469.2 10.4 %reduce-scatter.19.cloned.1.call-done = f32[256,768]{1,0:T(8,128)} async-done(((f32[512,768]{1,0:T(8,128)}), f32[256,768]{1,0:T(8,128)}) %reduce-scatter.19.cloned.1.call-update) | async-done | bytes 786448 | tf_op jit(solution)/shard_map/reduce_scatter | solution.py:232
  489.1 7.8 fusion.43
  504.3 8.1 fusion.42
  516.6 8.3 fusion.40
  528.7 7.8 fusion.41
  542.6 5.9 reduce-scatter.37.cloned.1.call-done
  586.7 4.7 multiply_reduce_fusion.3
  591.4 6.5 multiply_convert_fusion.3
  602.8 4.7 multiply_reduce_fusion.2
  607.5 5.0 multiply_convert_fusion.2
  615.0 8.1 multiply_reduce_fusion.1
  623.2 4.7 multiply_reduce_fusion
  628.0 45.8 %all_gather.77 = f32[16,2,8,384]{3,2,1,0:T(8,128)} all-gather(f32[1,2,8,384]{3,2,1,0:T(8,128)S(1)} %maximum_multiply_fusion), channel_id=1, replica_groups=mesh['dp'=16,'tensor'=2] {'dp'}, dimensions={0}, use_global_device_ids=true | all-gather | bytes 417792 | tf_op jit(solution)/shard_map/all_gather | solution.py:13
  677.5 40.4 %all_gather.78 = f32[16,2,8,384]{3,2,1,0:T(8,128)} all-gather(f32[1,2,8,384]{3,2,1,0:T(8,128)S(1)} %maximum_multiply_fusion.1), channel_id=1, replica_groups=mesh['dp'=16,'tensor'=2] {'dp'}, dimensions={0}, use_global_device_ids=true | all-gather | bytes 417792 | tf_op jit(solution)/shard_map/all_gather | solution.py:13
  717.8 6.7 multiply_convert_fusion.1
  726.3 4.7 multiply_convert_fusion
  747.9 42.9 %all_gather.79 = f32[16,2,8,384]{3,2,1,0:T(8,128)} all-gather(f32[1,2,8,384]{3,2,1,0:T(8,128)} %maximum_multiply_fusion.2), channel_id=1, replica_groups=mesh['dp'=16,'tensor'=2] {'dp'}, dimensions={0}, use_global_device_ids=true | all-gather | bytes 417792 | tf_op jit(solution)/shard_map/all_gather | solution.py:13
  803.8 37.8 %all_gather.160 = f32[16,2,8,384]{3,2,1,0:T(8,128)S(1)} all-gather(f32[1,2,8,384]{3,2,1,0:T(8,128)S(1)} %maximum_multiply_fusion.3), channel_id=1, replica_groups=mesh['dp'=16,'tensor'=2] {'dp'}, dimensions={0}, use_global_device_ids=true | all-gather | bytes 417792 | tf_op jit(solution)/shard_map/all_gather | solution.py:13
  (583 shorter events, 223.8 us)
Async XLA Ops:
  8.0 269.3 %reduce-scatter.21.cloned.1.call-start = ((), (), s32[]{:S(2)}) async-start(), calls=%async_computation.20 | async-start | bytes 2359296 | tf_op jit(solution)/shard_map/reduce_scatter | solution.py:213
  57.3 207.6 %copy-start.79 = (bf16[2,768,8]{1,2,0:T(8,128)(2,1)}, bf16[2,768,8]{1,2,0:T(8,128)(2,1)S(1)}, u32[]{:S(2)}) copy-start(bf16[2,768,8]{1,2,0:T(8,128)(2,1)S(1)} %copy.58) | copy-start | bytes 73732
  57.3 160.3 %copy-start.50 = (bf16[4,256,768]{2,1,0:T(8,128)(2,1)S(1)}, bf16[4,256,768]{2,1,0:T(8,128)(2,1)}, u32[]{:S(2)}) copy-start(bf16[4,256,768]{2,1,0:T(8,128)(2,1)} %param.17) | copy-start | bytes 4718596
  96.5 168.7 %copy-start.19 = (bf16[768,384]{1,0:T(8,128)(2,1)}, bf16[768,384]{1,0:T(8,128)(2,1)S(1)}, u32[]{:S(2)}) copy-start(bf16[768,384]{1,0:T(8,128)(2,1)S(1)} %all_gather.57) | copy-start | bytes 1769476
  137.6 130.3 %copy-start.14 = (bf16[768,384]{1,0:T(8,128)(2,1)}, bf16[768,384]{1,0:T(8,128)(2,1)S(1)}, u32[]{:S(2)}) copy-start(bf16[768,384]{1,0:T(8,128)(2,1)S(1)} %all_gather.58) | copy-start | bytes 1769476
  176.9 94.2 %copy-start.22 = (bf16[768,384]{1,0:T(8,128)(2,1)}, bf16[768,384]{1,0:T(8,128)(2,1)S(1)}, u32[]{:S(2)}) copy-start(bf16[768,384]{1,0:T(8,128)(2,1)S(1)} %all_gather.55) | copy-start | bytes 1769476
  217.7 56.5 %copy-start.24 = (bf16[384,768]{0,1:T(8,128)(2,1)}, bf16[384,768]{0,1:T(8,128)(2,1)S(1)}, u32[]{:S(2)}) copy-start(bf16[384,768]{0,1:T(8,128)(2,1)S(1)} %all_gather.59) | copy-start | bytes 1769476
  233.2 44.2 %reduce-scatter.17.cloned.1.call-start = ((), (), s32[]{:S(2)}) async-start(), calls=%async_computation.16 | async-start | bytes 2359296 | tf_op jit(solution)/shard_map/reduce_scatter | solution.py:213
  247.7 29.7 %reduce-scatter.29.cloned.1.call-start = ((), (), s32[]{:S(2)}) async-start(), calls=%async_computation.24 | async-start | bytes 2359296 | tf_op jit(solution)/shard_map/reduce_scatter | solution.py:213
  261.6 19.5 %reduce-scatter.25.cloned.1.call-start = ((), (), s32[]{:S(2)}) async-start(), calls=%async_computation.22 | async-start | bytes 2359296 | tf_op jit(solution)/shard_map/reduce_scatter | solution.py:213
  267.4 289.4 %copy-start.48 = (pred[512,512]{0,1:T(8,128)(4,1)}, pred[512,512]{0,1:T(8,128)(4,1)S(1)}, u32[]{:S(2)}) copy-start(pred[512,512]{0,1:T(8,128)(4,1)S(1)} %compare_and_fusion.1) | copy-start | bytes 786436
  271.0 285.8 %copy-start.125 = (f32[6,512]{1,0:T(8,128)}, f32[6,512]{1,0:T(8,128)S(1)}, u32[]{:S(2)}) copy-start(f32[6,512]{1,0:T(8,128)S(1)} %log_add_fusion.1) | copy-start | bytes 36868
  276.0 61.2 %all-gather.7.cloned.1.call-start = ((), (), s32[]{:S(2)}) async-start(), calls=%async_computation.17 | async-start | bytes 2506752 | tf_op jit(solution)/shard_map/all_gather | solution.py:358
  276.5 123.8 %all-gather.9.cloned.1.call-start = ((), (), s32[]{:S(2)}) async-start(), calls=%async_computation.18 | async-start | bytes 2506752 | tf_op jit(solution)/shard_map/all_gather | solution.py:359
  277.1 165.8 %reduce-scatter.31.cloned.1.call-start = ((), (), s32[]{:S(2)}) async-start(), calls=%async_computation.25 | async-start | bytes 2359296 | tf_op jit(solution)/shard_map/reduce_scatter | solution.py:232
  285.0 52.2 %copy-start.155 = (f32[1536]{0:T(1024)S(1)}, f32[1536]{0:T(1024)}, u32[]{:S(2)}) copy-start(f32[1536]{0:T(1024)} %param.28) | copy-start | bytes 18436
  285.5 163.4 %copy-start.139 = (f32[256]{0:T(256)}, f32[256]{0:T(256)S(1)}, u32[]{:S(2)}) copy-start(f32[256]{0:T(256)S(1)} %fusion.150) | copy-start | bytes 3076
  406.5 36.5 %reduce-scatter.27.cloned.1.call-start = ((), (), s32[]{:S(2)}) async-start(), calls=%async_computation.23 | async-start | bytes 2359296 | tf_op jit(solution)/shard_map/reduce_scatter | solution.py:232
  423.9 25.0 %reduce-scatter.23.cloned.1.call-start = ((), (), s32[]{:S(2)}) async-start(), calls=%async_computation.21 | async-start | bytes 2359296 | tf_op jit(solution)/shard_map/reduce_scatter | solution.py:232
  441.3 38.3 %reduce-scatter.19.cloned.1.call-start = ((), (), s32[]{:S(2)}) async-start(), calls=%async_computation.19 | async-start | bytes 2359296 | tf_op jit(solution)/shard_map/reduce_scatter | solution.py:232
  469.2 70.3 %reduce-scatter.45.cloned.1.call-start = ((), (), s32[]{:S(2)}) async-start(), calls=%async_computation.32 | async-start | bytes 2359296 | tf_op jit(solution)/shard_map/reduce_scatter | solution.py:274
  485.6 53.9 %copy-start.137 = (f32[256]{0:T(256)}, f32[256]{0:T(256)S(1)}, u32[]{:S(2)}) copy-start(f32[256]{0:T(256)S(1)} %negate_multiply_fusion.5) | copy-start | bytes 3076
  496.9 42.6 %reduce-scatter.41.cloned.1.call-start = ((), (), s32[]{:S(2)}) async-start(), calls=%async_computation.30 | async-start | bytes 2359296 | tf_op jit(solution)/shard_map/reduce_scatter | solution.py:274
  512.4 27.1 %reduce-scatter.33.cloned.1.call-start = ((), (), s32[]{:S(2)}) async-start(), calls=%async_computation.26 | async-start | bytes 2359296 | tf_op jit(solution)/shard_map/reduce_scatter | solution.py:274
  524.9 23.6 %reduce-scatter.37.cloned.1.call-start = ((), (), s32[]{:S(2)}) async-start(), calls=%async_computation.28 | async-start | bytes 2359296 | tf_op jit(solution)/shard_map/reduce_scatter | solution.py:274
  536.6 307.1 %reduce-scatter.35.cloned.1.call-start = ((), (), s32[]{:S(2)}) async-start(), calls=%async_computation.27 | async-start | bytes 1179648 | tf_op jit(solution)/shard_map/reduce_scatter | solution.py:302
  623.2 50.6 %copy-start.15 = (bf16[768,384]{1,0:T(8,128)(2,1)S(1)}, bf16[768,384]{1,0:T(8,128)(2,1)}, u32[]{:S(2)}) copy-start(bf16[768,384]{1,0:T(8,128)(2,1)} %copy-done.14) | copy-start | bytes 1769476
  623.2 51.2 %copy-start.80 = (bf16[2,768,8]{1,2,0:T(8,128)(2,1)S(1)}, bf16[2,768,8]{1,2,0:T(8,128)(2,1)}, u32[]{:S(2)}) copy-start(bf16[2,768,8]{1,2,0:T(8,128)(2,1)} %copy-done.79) | copy-start | bytes 73732
  677.4 168.4 %reduce-scatter.39.cloned.1.call-start = ((), (), s32[]{:S(2)}) async-start(), calls=%async_computation.29 | async-start | bytes 1179648 | tf_op jit(solution)/shard_map/reduce_scatter | solution.py:302
  738.9 109.0 %reduce-scatter.43.cloned.1.call-start = ((), (), s32[]{:S(2)}) async-start(), calls=%async_computation.31 | async-start | bytes 1179648 | tf_op jit(solution)/shard_map/reduce_scatter | solution.py:302
  747.8 51.2 %copy-start.11 = (bf16[6,512,512]{1,2,0:T(8,128)(2,1)S(1)}, bf16[6,512,512]{1,2,0:T(8,128)(2,1)}, u32[]{:S(2)}) copy-start(bf16[6,512,512]{1,2,0:T(8,128)(2,1)} %copy-done.10) | copy-start | bytes 9437188
  747.8 102.2 %reduce-scatter.47.cloned.1.call-start = ((), (), s32[]{:S(2)}) async-start(), calls=%async_computation.33 | async-start | bytes 1179648 | tf_op jit(solution)/shard_map/reduce_scatter | solution.py:302
  (152 other events, 1083.1 us)
Sparse Core Ops, SparseCore 0:
  233.3 4.9 reduce-scatter.20
  247.8 5.0 reduce-scatter.16
  261.7 5.0 reduce-scatter.28
  276.1 4.9 reduce-scatter.24
  406.6 7.4 reduce-scatter.30
  424.0 7.4 reduce-scatter.26
  441.4 7.4 reduce-scatter.22
  469.3 10.3 reduce-scatter.18
  497.0 10.3 reduce-scatter.44
  512.5 10.3 reduce-scatter.40
  525.7 10.3 reduce-scatter.32
  538.2 10.3 reduce-scatter.36
  677.5 4.0 reduce-scatter.34
  739.0 5.9 reduce-scatter.38
  748.0 8.3 reduce-scatter.42
  803.1 4.0 reduce-scatter.46
Sparse Core Ops, SparseCore 1:
  279.3 57.9 all-gather.6
  339.9 60.4 all-gather.8
